TPU v7x, 128 devices: a whole 4x4x4 slice. The times are simulated.
128 devices in a mesh: dp: 16 (over y, x_lo, core), shard: 8 (over z, x_hi).
Axes of the slice: x: 4 (x_hi: 2, x_lo: 2; x = x_hi * 2 + x_lo), y: 4, z: 4, core: 2. Of those that a mesh axis runs over, the one named last changes fastest.
Arguments:
- gradients: bfloat16 [16, 88, 512, 512], P('dp', 'shard'), may hold values from -60 to 60
- owners: int32 [8, 11], P('shard'), may hold values from 0 to 15, as said below
- block_param: int32 [88], replicated, may hold values from 0 to 6, never falling along the last dimension, each value on 1 to 25 neighbouring positions
- left_stat: float32 [32, 8, 512, 512], P('dp', 'shard'), may hold values from -4 to 8, as said below
- right_stat: float32 [32, 8, 512, 512], P('dp', 'shard'), may hold values from -4 to 8, as said below
- moment: float32 [32, 8, 512, 512], P('dp', 'shard'), may hold values from 0.5 to 50
- left_root: bfloat16 [32, 8, 512, 512], P('dp', 'shard'), may hold values from -1 to 3.5, as said below
- right_root: bfloat16 [32, 8, 512, 512], P('dp', 'shard'), may hold values from -1 to 3.5, as said below
Outputs:
- new_left: float32 [32, 8, 512, 512], P('dp', 'shard')
- new_right: float32 [32, 8, 512, 512], P('dp', 'shard')
- new_moment: float32 [32, 8, 512, 512], P('dp', 'shard')
- update: bfloat16 [88, 512, 512], P('shard')
Inputs may be any that keep to these rules, and one draw needn't show every extreme that they name: `owners`: in each row, no value occurs more than 2 times, and some value occurs exactly 2 times. `left_stat`: each slot's matrix is symmetric. `right_stat`: each slot's matrix is symmetric. `left_root`: each slot's matrix is symmetric. `right_root`: each slot's matrix is symmetric.
All inputs are finite; a program needn't handle non-finite values.
Results may differ from a plain program's by a relative error of at most 0.0058.
Values may be sent and summed in bfloat16 or wider, within the bound.
A program may use at most 192 MiB of HBM per device.

v0:
```python
import jax
import jax.numpy as jnp
from jax import lax
from jax.sharding import Mesh
from jax.sharding import PartitionSpec as P

NPARAM = 7
DP = ("dp_0", "dp_1", "dp_2")
SHARD = ("shard_0", "shard_1")
DP_SHARD = ("dp_0", "dp_1", "dp_2", "shard_0", "shard_1")
decay_rate = 0.95
tiny_value = 1e-06


def by_axis(x, axes):
    for axis in axes:
        x = lax.psum(x, axis)
    return x


def on_device(gradients, owners, block_param, left_stat, right_stat, moment, left_root, right_root):
    replicas = lax.axis_size(DP)
    capacity = left_stat.shape[0]
    blocks = gradients.shape[1]
    block_width = gradients.shape[3]
    device = lax.axis_index(DP)
    column = lax.axis_index(SHARD)
    owner_row = owners[0]
    counter = jnp.arange(blocks, dtype=jnp.int32)
    same_owner = owner_row[:, None] == owner_row[None, :]
    earlier = counter[None, :] < counter[:, None]
    places = owner_row * capacity + jnp.sum(jnp.where(same_owner & earlier, 1, 0), axis=1).astype(
        jnp.int32
    )
    slot_ids = jnp.arange(replicas * capacity, dtype=jnp.int32)
    matches = places[None, :] == slot_ids[:, None]
    source = jnp.min(jnp.where(matches, counter[None, :], blocks), axis=1)
    partials = gradients[0].astype(jnp.float32)
    row_share = lax.psum_scatter(partials, DP, scatter_dimension=1, tiled=True)
    share_padded = jnp.concatenate(
        [row_share, jnp.zeros((1,) + row_share.shape[1:], jnp.float32)], axis=0
    )
    outgoing = jnp.take(share_padded, source, axis=0).reshape(
        replicas, capacity, block_width // replicas, block_width
    )
    arrived = lax.all_to_all(outgoing, DP, split_axis=0, concat_axis=2, tiled=True)
    summed = arrived[0]
    left_gram = jnp.einsum("cij,ckj->cik", summed, summed, precision=lax.Precision.HIGHEST)
    right_gram = jnp.einsum("cji,cjk->cik", summed, summed, precision=lax.Precision.HIGHEST)
    new_left = decay_rate * left_stat + (1.0 - decay_rate) * left_gram[:, None]
    new_right = decay_rate * right_stat + (1.0 - decay_rate) * right_gram[:, None]
    new_moment = decay_rate * moment + (1.0 - decay_rate) * (summed * summed)[:, None]
    adam_step = summed / (jnp.sqrt(new_moment[:, 0]) + tiny_value)
    left_half = jnp.einsum(
        "cij,cjk->cik",
        left_root[:, 0],
        summed.astype(jnp.bfloat16),
        preferred_element_type=jnp.float32,
    ).astype(jnp.bfloat16)
    direction = jnp.einsum(
        "cij,cjk->cik", left_half, right_root[:, 0], preferred_element_type=jnp.float32
    )
    my_slots = lax.dynamic_slice_in_dim(matches, device * capacity, capacity, 0)
    local_params = lax.dynamic_slice_in_dim(block_param, column * blocks, blocks, 0)
    slot_param = jnp.sum(jnp.where(my_slots, local_params[None, :], 0), axis=1)
    is_live = jnp.any(my_slots, axis=1)
    param_ids = jnp.arange(NPARAM, dtype=jnp.int32)
    member = (slot_param[:, None] == param_ids[None, :]) & is_live[:, None]
    adam_squares = jnp.sum(adam_step * adam_step, axis=(1, 2))
    direction_squares = jnp.sum(direction * direction, axis=(1, 2))
    adam_local = jnp.sum(jnp.where(member, adam_squares[:, None], 0.0), axis=0)
    direction_local = jnp.sum(jnp.where(member, direction_squares[:, None], 0.0), axis=0)
    adam_norm, direction_norm = (by_axis(adam_local, DP_SHARD), by_axis(direction_local, DP_SHARD))
    graft_ratio = jnp.sqrt((adam_norm + tiny_value) / (direction_norm + tiny_value))
    slot_ratio = jnp.sum(jnp.where(member, graft_ratio[None, :], 0.0), axis=1)
    slot_update = (slot_ratio[:, None, None] * direction).astype(jnp.bfloat16)
    returned = lax.all_to_all(slot_update, DP, split_axis=1, concat_axis=0, tiled=True)
    pieces = jnp.take(returned, places, axis=0)
    update = lax.all_gather(pieces, DP, axis=1, tiled=True)
    return (new_left, new_right, new_moment, update)


def solution(mesh):
    finer = Mesh(
        mesh.devices.reshape(4, 2, 2, 4, 2), ("dp_0", "dp_1", "dp_2", "shard_0", "shard_1")
    )
    placed = (
        P(DP, SHARD, None, None),
        P(SHARD, None),
        P(),
        P(DP, SHARD, None, None),
        P(DP, SHARD, None, None),
        P(DP, SHARD, None, None),
        P(DP, SHARD, None, None),
        P(DP, SHARD, None, None),
    )
    return jax.shard_map(
        on_device,
        mesh=finer,
        in_specs=placed,
        out_specs=(
            P(DP, SHARD, None, None),
            P(DP, SHARD, None, None),
            P(DP, SHARD, None, None),
            P(SHARD, None, None),
        ),
        check_vma=False,
    )
```

profile of v0, /device:TPU:1, one launch (start us, length us, event | category | flops | bytes accessed | tf_op | source)
XLA Modules:
  0.0 309.6 jit_solution(17516869295652060086)
XLA Ops:
  7.2 8.7 %bitcast_convert_fusion = f32[11,512,512]{2,1,0:T(8,128)} fusion(bf16[1,11,512,512]{3,2,1,0:T(8,128)(2,1)} %param.8), kind=kLoop, calls=%fused_computation.2 | loop fusion | flops 2883584 | bytes 17301504 | tf_op jit(solution)/shard_map/convert_element_type | solution.py:38
  17.0 130.2 %reduce-scatter.2.cloned.1.call-done = f32[11,32,512]{2,1,0:T(8,128)} async-done(((f32[11,512,512]{2,1,0:T(8,128)}), f32[11,32,512]{2,1,0:T(8,128)}) %reduce-scatter.2.cloned.1.call-update) | async-done | bytes 720912 | tf_op jit(solution)/shard_map/reduce_scatter | solution.py:39
  147.2 1.2 concatenate.3
  148.4 2.0 gather_fusion
  150.4 3.1 %broadcast_select_fusion = f32[16,2,32,512]{3,2,1,0:T(8,128)} fusion(f32[16,2,32,512]{3,2,1,0:T(8,128)} %bitcast.83, pred[16,2]{1,0:T(8,128)(4,1)S(1)} %compare_and_fusion), kind=kLoop, calls=%fused_computation.23 | loop fusion | flops 524288 | bytes 4194336 | tf_op jit(solution)/shard_map/jit(_take)/select_n | solution.py:43
  153.5 5.9 %all-to-all-start = ((f32[16,2,32,512]{3,2,1,0:T(8,128)}), f32[16,2,32,512]{3,2,1,0:T(8,128)S(1)}, u32[]{:S(2)}, u32[]{:S(2)}) async-start(f32[16,2,32,512]{3,2,1,0:T(8,128)} %broadcast_select_fusion), calls=%async_computation.1 | async-start | bytes 4194304 | tf_op jit(solution)/shard_map/all_to_all | solution.py:46
  159.7 26.7 %all-to-all-done = f32[16,2,32,512]{3,2,1,0:T(8,128)S(1)} async-done(((f32[16,2,32,512]{3,2,1,0:T(8,128)}), f32[16,2,32,512]{3,2,1,0:T(8,128)S(1)}, u32[]{:S(2)}, u32[]{:S(2)}) %all-to-all-start) | async-done | bytes 2097184 | tf_op jit(solution)/shard_map/all_to_all | solution.py:46
  188.0 2.0 copy.61
  190.2 2.8 sqrt_add_fusion
  193.0 4.0 %multiply_reduce_fusion = (f32[2]{0:T(128)S(1)}, f32[2,512,512]{2,1,0:T(8,128)}) fusion(bf16[2,1,512,512]{3,2,1,0:T(8,128)(2,1)S(1)} %copy-done, bf16[2,1,512,512]{3,2,1,0:T(8,128)(2,1)} %param.14, f32[2,512,512]{2,1,0:T(8,128)S(1)} %bitcast.79), kind=kOutput, calls=%fused_computation.14 | convolution fusion | flops 1075838976 | bytes 6291464 | tf_op jit(solution)/shard_map/cij,cjk->cik/dot_general | solution.py:60
  197.0 2.7 fusion.3
  199.7 7.2 %all-reduce.2 = (f32[7]{0:T(128)S(1)}, f32[7]{0:T(128)S(1)}) all-reduce(f32[7]{0:T(128)S(1)} %get-tuple-element.25, f32[7]{0:T(128)S(1)} %get-tuple-element.24), channel_id=1, replica_groups=mesh['dp_0'=4,'dp_1'=2,'dp_2'=2,'shard_0'=4,'shard_1'=2] {'dp_0'}, use_global_device_ids=true, to_apply=%region_14.15 | all-reduce | flops 14 | bytes 112 | tf_op jit(solution)/shard_map/psum | solution.py:17
  206.9 3.8 %all-reduce.5 = (f32[7]{0:T(128)S(1)}, f32[7]{0:T(128)S(1)}) all-reduce(f32[7]{0:T(128)S(1)} %get-tuple-element.28, f32[7]{0:T(128)S(1)} %get-tuple-element.29), channel_id=1, replica_groups=mesh['dp_0'=4,'dp_1'=2,'dp_2'=2,'shard_0'=4,'shard_1'=2] {'dp_1'}, use_global_device_ids=true, to_apply=%region_15.16 | all-reduce | flops 14 | bytes 112 | tf_op jit(solution)/shard_map/psum | solution.py:17
  210.7 6.2 %all-reduce.4 = (f32[7]{0:T(128)S(1)}, f32[7]{0:T(128)S(1)}) all-reduce(f32[7]{0:T(128)S(1)} %get-tuple-element.34, f32[7]{0:T(128)S(1)} %get-tuple-element.35), channel_id=1, replica_groups=mesh['dp_0'=4,'dp_1'=2,'dp_2'=2,'shard_0'=4,'shard_1'=2] {'dp_2'}, use_global_device_ids=true, to_apply=%region_16.17 | all-reduce | flops 14 | bytes 112 | tf_op jit(solution)/shard_map/psum | solution.py:17
  216.9 8.7 %all-reduce.1 = (f32[7]{0:T(128)S(1)}, f32[7]{0:T(128)S(1)}) all-reduce(f32[7]{0:T(128)S(1)} %get-tuple-element.32, f32[7]{0:T(128)S(1)} %get-tuple-element.33), channel_id=1, replica_groups=mesh['dp_0'=4,'dp_1'=2,'dp_2'=2,'shard_0'=4,'shard_1'=2] {'shard_0'}, use_global_device_ids=true, to_apply=%region_17.18 | all-reduce | flops 14 | bytes 112 | tf_op jit(solution)/shard_map/psum | solution.py:17
  225.6 5.3 %all-reduce.3 = (f32[7]{0:T(128)S(1)}, f32[7]{0:T(128)S(1)}) all-reduce(f32[7]{0:T(128)S(1)} %get-tuple-element.26, f32[7]{0:T(128)S(1)} %get-tuple-element.27), channel_id=1, replica_groups=mesh['dp_0'=4,'dp_1'=2,'dp_2'=2,'shard_0'=4,'shard_1'=2] {'shard_1'}, use_global_device_ids=true, to_apply=%region_18.19 | all-reduce | flops 14 | bytes 112 | tf_op jit(solution)/shard_map/psum | solution.py:17
  231.1 1.9 multiply_convert_fusion
  233.0 2.0 copy.69
  235.0 7.0 %all-to-all-start.1 = ((bf16[2,512,512]{2,0,1:T(2,128)(2,1)}), bf16[2,512,512]{2,0,1:T(2,128)(2,1)S(1)}, u32[]{:S(2)}, u32[]{:S(2)}) async-start(bf16[2,512,512]{2,0,1:T(2,128)(2,1)} %copy.69), calls=%async_computation.2 | async-start | bytes 2097152 | tf_op jit(solution)/shard_map/all_to_all | solution.py:77
  242.2 15.5 %all-to-all-done.1 = bf16[2,512,512]{2,0,1:T(2,128)(2,1)S(1)} async-done(((bf16[2,512,512]{2,0,1:T(2,128)(2,1)}), bf16[2,512,512]{2,0,1:T(2,128)(2,1)S(1)}, u32[]{:S(2)}, u32[]{:S(2)}) %all-to-all-start.1) | async-done | bytes 1048608 | tf_op jit(solution)/shard_map/all_to_all | solution.py:77
  259.4 6.1 %fusion = f32[2,1,512,512]{3,2,1,0:T(8,128)} fusion(f32[2,1,512,512]{3,2,1,0:T(8,128)} %param.12, f32[2,512,512]{2,1,0:T(8,128)S(1)} %bitcast.80), kind=kOutput, calls=%fused_computation.6 | convolution fusion | flops 3222798336 | bytes 6291456 | tf_op jit(solution)/shard_map/cji,cjk->cik/dot_general | solution.py:49
  265.6 5.0 %fusion.1 = f32[2,1,512,512]{3,2,1,0:T(8,128)} fusion(f32[2,1,512,512]{3,2,1,0:T(8,128)S(1)} %copy-done.4, f32[2,512,512]{2,1,0:T(8,128)S(1)} %bitcast.81), kind=kOutput, calls=%fused_computation.9 | convolution fusion | flops 3222798336 | bytes 6291456 | tf_op jit(solution)/shard_map/cij,ckj->cik/dot_general | solution.py:48
  270.6 26.5 %all-gather.2.cloned.1.call-done = bf16[11,512,512]{2,1,0:T(8,128)(2,1)} async-done(((bf16[11,32,512]{2,1,0:T(8,128)(2,1)}), bf16[11,512,512]{2,1,0:T(8,128)(2,1)}) %all-gather.2.cloned.1.call-update) | async-done | bytes 5767184 | tf_op jit(solution)/shard_map/all_gather | solution.py:79
  297.1 5.6 %copy.85 = bf16[11,512,512]{2,1,0:T(8,128)(2,1)} copy(bf16[11,512,512]{2,1,0:T(8,128)(2,1)} %all-gather.2.cloned.1.call-done) | data formatting | bytes 11534336
  (41 shorter events, 5.4 us)
Async XLA Ops:
  7.2 185.8 %copy-start = (bf16[2,1,512,512]{3,2,1,0:T(8,128)(2,1)S(1)}, bf16[2,1,512,512]{3,2,1,0:T(8,128)(2,1)}, u32[]{:S(2)}) copy-start(bf16[2,1,512,512]{3,2,1,0:T(8,128)(2,1)} %param.15) | copy-start | bytes 3145732
  7.2 140.0 %reduce-scatter.2.cloned.1.call-start = ((), (), s32[]{:S(2)}) async-start(), calls=%async_computation.3 | async-start | bytes 12255232 | tf_op jit(solution)/shard_map/reduce_scatter | solution.py:39
  15.9 0.7 copy-start.6
  153.5 5.9 %copy-start.5 = (s32[88]{0:T(128)S(1)}, s32[88]{0:T(128)}, u32[]{:S(2)}) copy-start(s32[88]{0:T(128)} %param.10) | copy-start | bytes 1060
  153.5 32.9 %all-to-all-start = ((f32[16,2,32,512]{3,2,1,0:T(8,128)}), f32[16,2,32,512]{3,2,1,0:T(8,128)S(1)}, u32[]{:S(2)}, u32[]{:S(2)}) async-start(f32[16,2,32,512]{3,2,1,0:T(8,128)} %broadcast_select_fusion), calls=%async_computation.1 | async-start | bytes 4194304 | tf_op jit(solution)/shard_map/all_to_all | solution.py:46
  186.4 1.3 copy-start.2
  187.9 2.2 copy-start.3
  235.0 22.7 %all-to-all-start.1 = ((bf16[2,512,512]{2,0,1:T(2,128)(2,1)}), bf16[2,512,512]{2,0,1:T(2,128)(2,1)S(1)}, u32[]{:S(2)}, u32[]{:S(2)}) async-start(bf16[2,512,512]{2,0,1:T(2,128)(2,1)} %copy.69), calls=%async_computation.2 | async-start | bytes 2097152 | tf_op jit(solution)/shard_map/all_to_all | solution.py:77
  242.0 55.1 %all-gather.2.cloned.1.call-start = ((), (), s32[]{:S(2)}) async-start(), calls=%async_computation.4 | async-start | bytes 6127616 | tf_op jit(solution)/shard_map/all_gather | solution.py:79
  259.4 6.2 %copy-start.4 = (f32[2,1,512,512]{3,2,1,0:T(8,128)S(1)}, f32[2,1,512,512]{3,2,1,0:T(8,128)}, u32[]{:S(2)}) copy-start(f32[2,1,512,512]{3,2,1,0:T(8,128)} %param.11) | copy-start | bytes 6291460
  297.1 5.6 %copy-start.1 = (bf16[2,1,512,512]{3,2,1,0:T(8,128)(2,1)S(1)}, bf16[2,1,512,512]{3,2,1,0:T(8,128)(2,1)}, u32[]{:S(2)}) copy-start(bf16[2,1,512,512]{3,2,1,0:T(8,128)(2,1)} %param.15) | copy-start | bytes 3145732
Sparse Core Ops, SparseCore 0:
  16.0 131.0 reduce-scatter.1
  259.6 37.5 all-gather.1
where the time goes:
time: 310 us
  waiting for transfers between devices  199 us (64%)
  blocking collectives  31.1 us (10%)
  other arithmetic  21.1 us (7%)
  local copies, waits for them, and re-layouts  16 us (5%)
  matrix products  15.1 us (5%)
  between operations  14.2 us (5%)
  starting transfers between devices  13.1 us (4%)
    reduce_scatter x1, waiting for transfers between devices, on_device(): row_share = lax.psum_scatter(partials, DP, scatter_dimension=1, tiled=True)  130 us
    psum x5, blocking collectives, by_axis(): x = lax.psum(x, axis)  31.1 us
    all_to_all x1, waiting for transfers between devices, on_device(): lax.all_to_all(outgoing, DP, split_axis=0, concat_axis=2, tiled=True)  26.7 us
    all_gather x1, waiting for transfers between devices, on_device(): update = lax.all_gather(pieces, DP, axis=1, tiled=True)  26.5 us
    all_to_all x1, waiting for transfers between devices, on_device(): lax.all_to_all(slot_update, DP, split_axis=1, concat_axis=0, tiled=True)  15.5 us
    convert_element_type x1, other arithmetic, on_device(): partials = gradients[0].astype(jnp.float32)  8.67 us
    unnamed x15, local copies, waits for them, and re-layouts  7.59 us
    all_to_all x1, starting transfers between devices, on_device(): lax.all_to_all(slot_update, DP, split_axis=1, concat_axis=0, tiled=True)  6.96 us
  transfers between devices with their start and end apart: 4, of which 4 were waited for; matrix products, arithmetic and copies ran while one was open for 4% of the time, Pallas kernels for 0%

commit v1 on v0

--- a/solution.py
+++ b/solution.py
@@ -76,7 +76,7 @@
     slot_update = (slot_ratio[:, None, None] * direction).astype(jnp.bfloat16)
     returned = lax.all_to_all(slot_update, DP, split_axis=1, concat_axis=0, tiled=True)
     pieces = jnp.take(returned, places, axis=0)
-    update = lax.all_gather(pieces, DP, axis=1, tiled=True)
+    update = jnp.concatenate(lax.all_gather(pieces, axis_name=DP), axis=1)
     return (new_left, new_right, new_moment, update)
 
 

time: 310 us -> 311 us (level)
    all_gather x0 -> x1, local copies, waits for them, and re-layouts: none -> 6.24 us  [on_device(): update = jnp.concatenate(lax.all_gather(pieces, axis_name=DP), axis=1)]
    unnamed x15 -> x14, local copies, waits for them, and re-layouts: 7.59 us -> 1.97 us
where the time goes in v1:
time: 311 us; the launch traced here: 310 us
  waiting for transfers between devices  199 us (64%)
  blocking collectives  31.1 us (10%)
  other arithmetic  21.1 us (7%)
  local copies, waits for them, and re-layouts  16.6 us (5%)
  matrix products  15.1 us (5%)
  between operations  14.2 us (5%)
  starting transfers between devices  13.1 us (4%)
    reduce_scatter x1, waiting for transfers between devices, on_device(): row_share = lax.psum_scatter(partials, DP, scatter_dimension=1, tiled=True)  130 us
    psum x5, blocking collectives, by_axis(): x = lax.psum(x, axis)  31.1 us
    all_to_all x1, waiting for transfers between devices, on_device(): lax.all_to_all(outgoing, DP, split_axis=0, concat_axis=2, tiled=True)  26.7 us
    all_gather x1, waiting for transfers between devices, on_device(): update = jnp.concatenate(lax.all_gather(pieces, axis_name=DP), axis=1)  26.5 us
    all_to_all x1, waiting for transfers between devices, on_device(): lax.all_to_all(slot_update, DP, split_axis=1, concat_axis=0, tiled=True)  15.5 us
    convert_element_type x1, other arithmetic, on_device(): partials = gradients[0].astype(jnp.float32)  8.67 us
    all_to_all x1, starting transfers between devices, on_device(): lax.all_to_all(slot_update, DP, split_axis=1, concat_axis=0, tiled=True)  6.96 us
    all_gather x1, local copies, waits for them, and re-layouts, on_device(): update = jnp.concatenate(lax.all_gather(pieces, axis_name=DP), axis=1)  6.24 us
  transfers between devices with their start and end apart: 4, of which 4 were waited for; matrix products, arithmetic and copies ran while one was open for 4% of the time, Pallas kernels for 0%

profile of v1, /device:TPU:1, one launch (start us, length us, event | category | flops | bytes accessed | tf_op | source)
XLA Modules:
  0.0 310.2 jit_solution(6380251107127345327)
XLA Ops:
  7.2 8.7 %bitcast_convert_fusion = f32[11,512,512]{2,1,0:T(8,128)} fusion(bf16[1,11,512,512]{3,2,1,0:T(8,128)(2,1)} %param.8), kind=kLoop, calls=%fused_computation.2 | loop fusion | flops 2883584 | bytes 17301504 | tf_op jit(solution)/shard_map/convert_element_type | solution.py:38
  17.0 130.2 %reduce-scatter.2.cloned.1.call-done = f32[11,32,512]{2,1,0:T(8,128)} async-done(((f32[11,512,512]{2,1,0:T(8,128)}), f32[11,32,512]{2,1,0:T(8,128)}) %reduce-scatter.2.cloned.1.call-update) | async-done | bytes 720912 | tf_op jit(solution)/shard_map/reduce_scatter | solution.py:39
  147.2 1.2 concatenate.3
  148.4 2.0 gather_fusion
  150.4 3.1 %broadcast_select_fusion = f32[16,2,32,512]{3,2,1,0:T(8,128)} fusion(f32[16,2,32,512]{3,2,1,0:T(8,128)} %bitcast.88, pred[16,2]{1,0:T(8,128)(4,1)S(1)} %compare_and_fusion), kind=kLoop, calls=%fused_computation.23 | loop fusion | flops 524288 | bytes 4194336 | tf_op jit(solution)/shard_map/jit(_take)/select_n | solution.py:43
  153.5 5.9 %all-to-all-start = ((f32[16,2,32,512]{3,2,1,0:T(8,128)}), f32[16,2,32,512]{3,2,1,0:T(8,128)S(1)}, u32[]{:S(2)}, u32[]{:S(2)}) async-start(f32[16,2,32,512]{3,2,1,0:T(8,128)} %broadcast_select_fusion), calls=%async_computation.1 | async-start | bytes 4194304 | tf_op jit(solution)/shard_map/all_to_all | solution.py:46
  159.7 26.7 %all-to-all-done = f32[16,2,32,512]{3,2,1,0:T(8,128)S(1)} async-done(((f32[16,2,32,512]{3,2,1,0:T(8,128)}), f32[16,2,32,512]{3,2,1,0:T(8,128)S(1)}, u32[]{:S(2)}, u32[]{:S(2)}) %all-to-all-start) | async-done | bytes 2097184 | tf_op jit(solution)/shard_map/all_to_all | solution.py:46
  188.0 2.0 copy.76
  190.2 2.8 sqrt_add_fusion
  193.0 4.0 %multiply_reduce_fusion = (f32[2]{0:T(128)S(1)}, f32[2,512,512]{2,1,0:T(8,128)}) fusion(bf16[2,1,512,512]{3,2,1,0:T(8,128)(2,1)S(1)} %copy-done, bf16[2,1,512,512]{3,2,1,0:T(8,128)(2,1)} %param.14, f32[2,512,512]{2,1,0:T(8,128)S(1)} %bitcast.84), kind=kOutput, calls=%fused_computation.14 | convolution fusion | flops 1075838976 | bytes 6291464 | tf_op jit(solution)/shard_map/cij,cjk->cik/dot_general | solution.py:60
  197.0 2.7 fusion.3
  199.7 7.2 %all-reduce.2 = (f32[7]{0:T(128)S(1)}, f32[7]{0:T(128)S(1)}) all-reduce(f32[7]{0:T(128)S(1)} %get-tuple-element.29, f32[7]{0:T(128)S(1)} %get-tuple-element.28), channel_id=1, replica_groups=mesh['dp_0'=4,'dp_1'=2,'dp_2'=2,'shard_0'=4,'shard_1'=2] {'dp_0'}, use_global_device_ids=true, to_apply=%region_14.15 | all-reduce | flops 14 | bytes 112 | tf_op jit(solution)/shard_map/psum | solution.py:17
  206.9 3.8 %all-reduce.5 = (f32[7]{0:T(128)S(1)}, f32[7]{0:T(128)S(1)}) all-reduce(f32[7]{0:T(128)S(1)} %get-tuple-element.32, f32[7]{0:T(128)S(1)} %get-tuple-element.33), channel_id=1, replica_groups=mesh['dp_0'=4,'dp_1'=2,'dp_2'=2,'shard_0'=4,'shard_1'=2] {'dp_1'}, use_global_device_ids=true, to_apply=%region_15.16 | all-reduce | flops 14 | bytes 112 | tf_op jit(solution)/shard_map/psum | solution.py:17
  210.7 6.2 %all-reduce.4 = (f32[7]{0:T(128)S(1)}, f32[7]{0:T(128)S(1)}) all-reduce(f32[7]{0:T(128)S(1)} %get-tuple-element.38, f32[7]{0:T(128)S(1)} %get-tuple-element.39), channel_id=1, replica_groups=mesh['dp_0'=4,'dp_1'=2,'dp_2'=2,'shard_0'=4,'shard_1'=2] {'dp_2'}, use_global_device_ids=true, to_apply=%region_16.17 | all-reduce | flops 14 | bytes 112 | tf_op jit(solution)/shard_map/psum | solution.py:17
  216.9 8.7 %all-reduce.1 = (f32[7]{0:T(128)S(1)}, f32[7]{0:T(128)S(1)}) all-reduce(f32[7]{0:T(128)S(1)} %get-tuple-element.36, f32[7]{0:T(128)S(1)} %get-tuple-element.37), channel_id=1, replica_groups=mesh['dp_0'=4,'dp_1'=2,'dp_2'=2,'shard_0'=4,'shard_1'=2] {'shard_0'}, use_global_device_ids=true, to_apply=%region_17.18 | all-reduce | flops 14 | bytes 112 | tf_op jit(solution)/shard_map/psum | solution.py:17
  225.6 5.3 %all-reduce.3 = (f32[7]{0:T(128)S(1)}, f32[7]{0:T(128)S(1)}) all-reduce(f32[7]{0:T(128)S(1)} %get-tuple-element.30, f32[7]{0:T(128)S(1)} %get-tuple-element.31), channel_id=1, replica_groups=mesh['dp_0'=4,'dp_1'=2,'dp_2'=2,'shard_0'=4,'shard_1'=2] {'shard_1'}, use_global_device_ids=true, to_apply=%region_18.19 | all-reduce | flops 14 | bytes 112 | tf_op jit(solution)/shard_map/psum | solution.py:17
  231.1 1.9 multiply_convert_fusion
  233.0 2.0 copy.84
  235.0 7.0 %all-to-all-start.1 = ((bf16[2,512,512]{2,0,1:T(2,128)(2,1)}), bf16[2,512,512]{2,0,1:T(2,128)(2,1)S(1)}, u32[]{:S(2)}, u32[]{:S(2)}) async-start(bf16[2,512,512]{2,0,1:T(2,128)(2,1)} %copy.84), calls=%async_computation.2 | async-start | bytes 2097152 | tf_op jit(solution)/shard_map/all_to_all | solution.py:77
  242.2 15.5 %all-to-all-done.1 = bf16[2,512,512]{2,0,1:T(2,128)(2,1)S(1)} async-done(((bf16[2,512,512]{2,0,1:T(2,128)(2,1)}), bf16[2,512,512]{2,0,1:T(2,128)(2,1)S(1)}, u32[]{:S(2)}, u32[]{:S(2)}) %all-to-all-start.1) | async-done | bytes 1048608 | tf_op jit(solution)/shard_map/all_to_all | solution.py:77
  259.4 6.1 %fusion = f32[2,1,512,512]{3,2,1,0:T(8,128)} fusion(f32[2,1,512,512]{3,2,1,0:T(8,128)} %param.12, f32[2,512,512]{2,1,0:T(8,128)S(1)} %bitcast.85), kind=kOutput, calls=%fused_computation.6 | convolution fusion | flops 3222798336 | bytes 6291456 | tf_op jit(solution)/shard_map/cji,cjk->cik/dot_general | solution.py:49
  265.6 5.0 %fusion.1 = f32[2,1,512,512]{3,2,1,0:T(8,128)} fusion(f32[2,1,512,512]{3,2,1,0:T(8,128)S(1)} %copy-done.4, f32[2,512,512]{2,1,0:T(8,128)S(1)} %bitcast.86), kind=kOutput, calls=%fused_computation.9 | convolution fusion | flops 3222798336 | bytes 6291456 | tf_op jit(solution)/shard_map/cij,ckj->cik/dot_general | solution.py:48
  270.6 26.5 %all-gather.2.cloned.1.call-done = bf16[16,11,32,512]{3,2,1,0:T(8,128)(2,1)} async-done(((bf16[1,11,32,512]{3,2,1,0:T(8,128)(2,1)}), bf16[16,11,32,512]{3,2,1,0:T(8,128)(2,1)}) %all-gather.2.cloned.1.call-update) | async-done | bytes 5767184 | tf_op jit(solution)/shard_map/all_gather | solution.py:79
  297.1 6.2 %copy.87 = bf16[16,11,32,512]{3,2,0,1:T(8,128)(2,1)} copy(bf16[16,11,32,512]{3,2,1,0:T(8,128)(2,1)} %all-gather.2.cloned.1.call-done) | data formatting | bytes 11534336 | tf_op jit(solution)/shard_map/all_gather | solution.py:79
  (41 shorter events, 5.4 us)
Async XLA Ops:
  7.2 185.8 %copy-start = (bf16[2,1,512,512]{3,2,1,0:T(8,128)(2,1)S(1)}, bf16[2,1,512,512]{3,2,1,0:T(8,128)(2,1)}, u32[]{:S(2)}) copy-start(bf16[2,1,512,512]{3,2,1,0:T(8,128)(2,1)} %param.15) | copy-start | bytes 3145732
  7.2 140.0 %reduce-scatter.2.cloned.1.call-start = ((), (), s32[]{:S(2)}) async-start(), calls=%async_computation.3 | async-start | bytes 12255232 | tf_op jit(solution)/shard_map/reduce_scatter | solution.py:39
  15.9 0.7 copy-start.6
  153.5 5.9 %copy-start.5 = (s32[88]{0:T(128)S(1)}, s32[88]{0:T(128)}, u32[]{:S(2)}) copy-start(s32[88]{0:T(128)} %param.10) | copy-start | bytes 1060
  153.5 32.9 %all-to-all-start = ((f32[16,2,32,512]{3,2,1,0:T(8,128)}), f32[16,2,32,512]{3,2,1,0:T(8,128)S(1)}, u32[]{:S(2)}, u32[]{:S(2)}) async-start(f32[16,2,32,512]{3,2,1,0:T(8,128)} %broadcast_select_fusion), calls=%async_computation.1 | async-start | bytes 4194304 | tf_op jit(solution)/shard_map/all_to_all | solution.py:46
  186.4 1.3 copy-start.2
  187.9 2.2 copy-start.3
  235.0 22.7 %all-to-all-start.1 = ((bf16[2,512,512]{2,0,1:T(2,128)(2,1)}), bf16[2,512,512]{2,0,1:T(2,128)(2,1)S(1)}, u32[]{:S(2)}, u32[]{:S(2)}) async-start(bf16[2,512,512]{2,0,1:T(2,128)(2,1)} %copy.84), calls=%async_computation.2 | async-start | bytes 2097152 | tf_op jit(solution)/shard_map/all_to_all | solution.py:77
  242.0 55.1 %all-gather.2.cloned.1.call-start = ((), (), s32[]{:S(2)}) async-start(), calls=%async_computation.4 | async-start | bytes 6127616 | tf_op jit(solution)/shard_map/all_gather | solution.py:79
  259.4 6.2 %copy-start.4 = (f32[2,1,512,512]{3,2,1,0:T(8,128)S(1)}, f32[2,1,512,512]{3,2,1,0:T(8,128)}, u32[]{:S(2)}) copy-start(f32[2,1,512,512]{3,2,1,0:T(8,128)} %param.11) | copy-start | bytes 6291460
  297.1 6.2 %copy-start.1 = (bf16[2,1,512,512]{3,2,1,0:T(8,128)(2,1)S(1)}, bf16[2,1,512,512]{3,2,1,0:T(8,128)(2,1)}, u32[]{:S(2)}) copy-start(bf16[2,1,512,512]{3,2,1,0:T(8,128)(2,1)} %param.15) | copy-start | bytes 3145732
Sparse Core Ops, SparseCore 0:
  16.0 131.0 reduce-scatter.1
  259.6 37.5 all-gather.1
